TPU v7x, 128 devices: a whole 4x4x4 slice. The times are simulated.
128 devices in a mesh: src: 16 (over z, x), rcv: 8 (over y, core).
Axes of the slice: x: 4, y: 4, z: 4, core: 2. Of those that a mesh axis runs over, the one named last changes fastest.
Arguments:
- traces: bfloat16 [2, 2, 2048, 2048], P(None, None, 'src', 'rcv'), may hold values from -8 to 8
- wavelet: float32 [2, 2], replicated, may hold values from -0.3 to 0.3
Outputs:
- coeffs: float32 [2, 2, 2048, 2048], P(None, None, 'src', 'rcv')
- norms: float32 [2, 2], replicated
All inputs are finite; a program needn't handle non-finite values.
Results may differ from a plain program's by a relative error of at most 0.006.
Values may be sent and summed in bfloat16 or wider, within the bound.
A program may use at most 128 MiB of HBM per device.

v0:
```python
import math
import jax
import jax.numpy as jnp
from jax import lax
from jax.sharding import Mesh
from jax.sharding import PartitionSpec as P

ITERS = 2
SRC = ("src_0", "src_1")
RCV = ("rcv_0", "rcv_1")
SRC_RCV = ("src_0", "src_1", "rcv_0", "rcv_1")
step_length = 0.4
shrink_fraction = 0.2


def laid_out(tiles, dim):
    shape = list(tiles.shape[1:])
    shape[dim] *= tiles.shape[0]
    return jnp.moveaxis(tiles, 0, dim).reshape(shape)


def copy_for_each(x, axis):
    copies = jnp.broadcast_to(x, (lax.axis_size(axis), *x.shape))
    return lax.all_to_all(copies, axis, split_axis=0, concat_axis=0, tiled=True)


def gathered_copies(x, axis, dim):
    return laid_out(copy_for_each(x, axis), dim)


def all_in_one(x, axis):
    leaves = jax.tree.leaves(x)
    order = sorted(range(len(leaves)), key=lambda k: -leaves[k].size)
    width = (1, *leaves[order[0]].shape)[-1]
    lines = [
        jnp.pad(leaves[k].reshape(-1), (0, -leaves[k].size % width)).reshape(-1, width)
        for k in order
    ]
    both, at, found = (lax.all_gather(jnp.concatenate(lines), axis), 0, {})
    for k, line in zip(order, lines):
        share = both[:, at : at + len(line)].reshape(len(both), -1)
        found[k] = share[:, : leaves[k].size].reshape(-1, *leaves[k].shape)
        at += len(line)
    numbers = iter(range(len(leaves)))
    return jax.tree.map(lambda _: found[next(numbers)], x)


def once_a_type(x, axis):
    leaves, found = (jax.tree.leaves(x), {})
    for first, a in enumerate(leaves):
        if first not in found:
            alike = [k for k, b in enumerate(leaves) if b.dtype == a.dtype]
            got = (
                all_in_one([leaves[k] for k in alike], axis)
                if len(alike) > 1
                else [lax.all_gather(a, axis)]
            )
            for k, b in zip(alike, got):
                found[k] = b
    numbers = iter(range(len(leaves)))
    return jax.tree.map(lambda _: found[next(numbers)], x)


def joined_all(x, axes, combine):
    for axis in axes:
        pieces = once_a_type(x, axis)
        x = jax.tree.map(lambda part: part[0], pieces)
        for k in range(1, lax.axis_size(axis)):
            x = combine(x, jax.tree.map(lambda part: part[k], pieces))
    return x


def table_block(offset, height, second, breadth, length, direction):
    left_index = offset + jnp.arange(height, dtype=jnp.int32)
    right_index = second + jnp.arange(breadth, dtype=jnp.int32)
    phase = left_index[:, None] * right_index[None, :] % length
    angle = phase.astype(jnp.float32) * (2.0 * math.pi / length)
    scale = 1.0 / math.sqrt(length)
    return jnp.stack([jnp.cos(angle) * scale, direction * (jnp.sin(angle) * scale)]).astype(
        jnp.bfloat16
    )


def complex_product(left_side, right_side, pattern, left_table, right_table):
    left_re = left_side[0] if left_table else left_side[:, 0]
    left_im = left_side[1] if left_table else left_side[:, 1]
    right_re = right_side[0] if right_table else right_side[:, 0]
    right_im = right_side[1] if right_table else right_side[:, 1]

    def single(first_op, second_op):
        return jnp.einsum(pattern, first_op, second_op, preferred_element_type=jnp.float32)

    real_part = single(left_re, right_re) - single(left_im, right_im)
    imag_part = single(left_re, right_im) + single(left_im, right_re)
    return jnp.stack([real_part, imag_part], axis=1)


def complex_scale(real_part, imag_part, values):
    return jnp.stack(
        [
            real_part * values[:, 0] - imag_part * values[:, 1],
            real_part * values[:, 1] + imag_part * values[:, 0],
        ],
        axis=1,
    )


def combine_stats(first_pair, second_pair):
    return (jnp.maximum(first_pair[0], second_pair[0]), first_pair[1] + second_pair[1])


def per_device(traces, wavelet):
    row_count = traces.shape[2]
    col_count = traces.shape[3]
    extent = row_count * lax.axis_size(SRC)
    row_anchor = lax.axis_index(SRC) * row_count
    col_anchor = lax.axis_index(RCV) * col_count
    root_scale = 1.0 / math.sqrt(extent)
    wave_re = (wavelet[:, 0] * root_scale)[:, None, None]
    wave_im = (wavelet[:, 1] * root_scale)[:, None, None]
    forward_cols = table_block(0, extent, col_anchor, col_count, extent, -1.0)
    forward_rows = table_block(row_anchor, row_count, 0, extent, extent, -1.0)
    inverse_cols = table_block(0, extent, col_anchor, col_count, extent, 1.0)
    inverse_rows = table_block(row_anchor, row_count, 0, extent, extent, 1.0)
    coeffs = jnp.zeros(traces.shape, jnp.float32)
    columns_all = lax.all_gather(traces, SRC, axis=2, tiled=True)
    traces_f = traces.astype(jnp.float32)

    def column_section(table, portion):
        return complex_product(table, portion, "mn,fnc->fmc", True, False)

    def paired(first_op, second_op):
        return jnp.einsum("fmr,fkr->fmk", first_op, second_op, preferred_element_type=jnp.float32)

    norm_list = []
    for iteration in range(ITERS):
        if iteration == 0:
            misfit = traces_f
        else:
            coeff_half = coeffs.astype(jnp.bfloat16)
            halfway = column_section(
                inverse_rows, lax.all_gather(coeff_half, SRC, axis=2, tiled=True)
            ).astype(jnp.bfloat16)
            model = complex_product(
                gathered_copies(halfway, RCV, 3), inverse_cols, "fmn,nc->fmc", False, True
            ).astype(jnp.bfloat16)
            product = complex_product(
                gathered_copies(model, RCV, 3), columns_all, "fmn,fnc->fmc", False, False
            )
            misfit = traces_f - model.astype(jnp.float32) + complex_scale(wave_re, wave_im, product)
        local_squares = jnp.sum(misfit * misfit, axis=(1, 2, 3))
        misfit_half = misfit.astype(jnp.bfloat16)
        misfit_re = misfit_half[:, 0]
        misfit_im = misfit_half[:, 1]
        column_re = columns_all[:, 0]
        column_im = columns_all[:, 1]
        back_re = paired(misfit_re, column_re) + paired(misfit_im, column_re * 0 + column_im)
        back_im = paired(misfit_im, column_re) - paired(misfit_re, column_im)
        scaled = complex_scale(wave_re, -wave_im, jnp.stack([back_re, back_im], axis=1))
        embedded = lax.dynamic_update_slice(
            jnp.zeros_like(scaled), misfit_half.astype(jnp.float32), (0, 0, 0, col_anchor)
        )
        gradient_rows = lax.psum(embedded - scaled, RCV)
        halfway = complex_product(
            gradient_rows.astype(jnp.bfloat16), forward_cols, "fmn,nc->fmc", False, True
        ).astype(jnp.bfloat16)
        spectrum = column_section(forward_rows, lax.all_gather(halfway, SRC, axis=2, tiled=True))
        trial = coeffs + step_length * spectrum
        magnitude = jnp.sqrt(trial[:, 0] * trial[:, 0] + trial[:, 1] * trial[:, 1])
        local_peak = jnp.max(magnitude, axis=(1, 2))
        global_peak, total_squares = joined_all((local_peak, local_squares), SRC_RCV, combine_stats)
        norm_list.append(jnp.sqrt(total_squares))
        level = shrink_fraction * global_peak[:, None, None]
        factor = jnp.maximum(1.0 - level / jnp.maximum(magnitude, level), 0.0)
        coeffs = trial * factor[:, None]
    return (coeffs, jnp.stack(norm_list))


def solution(mesh):
    split = Mesh(mesh.devices.reshape(4, 4, 4, 2), ("src_0", "src_1", "rcv_0", "rcv_1"))
    return jax.shard_map(
        per_device,
        mesh=split,
        in_specs=(P(None, None, SRC, RCV), P()),
        out_specs=(P(None, None, SRC, RCV), P()),
        check_vma=False,
    )
```

profile of v0, /device:TPU:1, one launch (start us, length us, event | category | flops | bytes accessed | tf_op | source)
XLA Modules:
  0.0 641.2 jit_solution(3735553232752024656)
XLA Ops:
  7.2 1.7 copy.19
  10.0 2.5 broadcast.426.clone
  13.3 51.9 %all-gather.21.cloned.1.call-done = bf16[2,2,2048,256]{3,2,0,1:T(8,128)(2,1)} async-done(((bf16[2,2,128,256]{3,2,0,1:T(8,128)(2,1)}), bf16[2,2,2048,256]{3,2,0,1:T(8,128)(2,1)}) %all-gather.21.cloned.1.call-update) | async-done | bytes 4194320 | tf_op jit(solution)/shard_map/all_gather | solution.py:126
  65.3 2.5 fusion.78
  69.7 1.0 subtract_bitcast_fusion.1
  70.7 5.0 maximum_subtract_fusion
  75.7 56.5 %all-reduce.2 = bf16[2,2,128,2048]{3,2,0,1:T(8,128)(2,1)S(1)} all-reduce(f32[2,2,128,2048]{3,2,0,1:T(8,128)} %maximum_subtract_fusion), channel_id=1, replica_groups=mesh['src_0'=4,'src_1'=4,'rcv_0'=4,'rcv_1'=2] {'rcv_0','rcv_1'}, use_global_device_ids=true, to_apply=%region_0.1 | all-reduce | flops 1048576 | bytes 6291456 | tf_op jit(solution)/shard_map/psum | solution.py:163
  132.2 7.9 %fusion.62 = f32[2,128,256]{2,1,0:T(8,128)S(1)} fusion(s32[256]{0:T(256)S(1)} %iota_add_fusion, bf16[2,2,128,2048]{3,2,0,1:T(8,128)(2,1)S(1)} %all-reduce.2), kind=kOutput, calls=%fused_computation.104 | convolution fusion | flops 276824064 | bytes 1311744 | tf_op jit(solution)/shard_map/fmn,nc->fmc/dot_general | solution.py:91
  140.1 8.1 %fusion.67 = f32[2,128,256]{2,1,0:T(8,128)S(1)} fusion(s32[256]{0:T(256)S(1)} %iota_add_fusion, bf16[2,2,128,2048]{3,2,0,1:T(8,128)(2,1)S(1)} %all-reduce.2), kind=kOutput, calls=%fused_computation.106 | convolution fusion | flops 276824064 | bytes 1311744 | tf_op jit(solution)/shard_map/fmn,nc->fmc/dot_general | solution.py:91
  148.3 8.2 %fusion.44 = bf16[2,1,128,256]{3,2,0,1:T(8,128)(2,1)S(1)} fusion(f32[2,128,256]{2,1,0:T(8,128)S(1)} %fusion.62, s32[256]{0:T(256)S(1)} %iota_add_fusion, bf16[2,2,128,2048]{3,2,0,1:T(8,128)(2,1)S(1)} %all-reduce.2), kind=kOutput, calls=%fused_computation.80 | convolution fusion | flops 276955136 | bytes 1442816 | tf_op jit(solution)/shard_map/fmn,nc->fmc/dot_general | solution.py:91
  156.4 7.9 %fusion.43 = bf16[2,1,128,256]{3,2,0,1:T(8,128)(2,1)S(1)} fusion(f32[2,128,256]{2,1,0:T(8,128)S(1)} %fusion.67, s32[256]{0:T(256)S(1)} %iota_add_fusion, bf16[2,2,128,2048]{3,2,0,1:T(8,128)(2,1)S(1)} %all-reduce.2), kind=kOutput, calls=%fused_computation.79 | convolution fusion | flops 276955136 | bytes 1442816 | tf_op jit(solution)/shard_map/fmn,nc->fmc/dot_general | solution.py:91
  165.5 51.1 %all-gather.23.cloned.1.call-done = bf16[2,2,2048,256]{3,2,0,1:T(8,128)(2,1)} async-done(((bf16[2,2,128,256]{3,2,0,1:T(8,128)(2,1)}), bf16[2,2,2048,256]{3,2,0,1:T(8,128)(2,1)}) %all-gather.23.cloned.1.call-update) | async-done | bytes 4194320 | tf_op jit(solution)/shard_map/all_gather | solution.py:167
  216.7 6.0 fusion.8
  222.7 4.3 fusion.7
  227.0 4.5 fusion.26
  231.5 4.3 fusion.28
  236.0 7.6 %all-gather.8 = f32[4,2,2]{2,1,0:T(2,128)S(1)} all-gather(f32[1,2,2]{2,1,0:T(2,128)S(1)} %maximum_bitcast_fusion.1), channel_id=2, replica_groups=mesh['src_0'=4,'src_1'=4,'rcv_0'=4,'rcv_1'=2] {'src_0'}, dimensions={0}, use_global_device_ids=true | all-gather | bytes 80 | tf_op jit(solution)/shard_map/all_gather | solution.py:39
  243.7 5.9 all-gather.9
  249.6 7.8 %all-gather.10 = f32[4,2,2]{2,1,0:T(2,128)S(1)} all-gather(f32[1,2,2]{2,1,0:T(2,128)S(1)} %maximum_bitcast_fusion.3), channel_id=4, replica_groups=mesh['src_0'=4,'src_1'=4,'rcv_0'=4,'rcv_1'=2] {'rcv_0'}, dimensions={0}, use_global_device_ids=true | all-gather | bytes 80 | tf_op jit(solution)/shard_map/all_gather | solution.py:39
  257.4 8.2 %all-gather.11 = f32[2,2,2]{2,1,0:T(2,128)S(1)} all-gather(f32[1,2,2]{2,1,0:T(2,128)S(1)} %maximum_bitcast_fusion.4), channel_id=5, replica_groups=mesh['src_0'=4,'src_1'=4,'rcv_0'=4,'rcv_1'=2] {'rcv_1'}, dimensions={0}, use_global_device_ids=true | all-gather | bytes 48 | tf_op jit(solution)/shard_map/all_gather | solution.py:39
  267.0 50.0 %all-gather.25.cloned.1.call-done = bf16[2,2,2048,256]{2,3,0,1:T(8,128)(2,1)} async-done(((bf16[2,2,128,256]{2,3,0,1:T(8,128)(2,1)}), bf16[2,2,2048,256]{2,3,0,1:T(8,128)(2,1)}) %all-gather.25.cloned.1.call-update) | async-done | bytes 4194320 | tf_op jit(solution)/shard_map/all_gather | solution.py:142
  317.0 6.1 fusion.12
  323.1 4.4 fusion.11
  327.5 4.6 fusion.37
  332.1 4.4 fusion.38
  336.9 32.3 %all_to_all.10 = bf16[8,2,2,128,256]{4,3,1,2,0:T(8,128)(2,1)S(1)} all-to-all(bf16[8,2,2,128,256]{4,3,1,2,0:T(8,128)(2,1)S(1)} %broadcast_in_dim.4), channel_id=1, replica_groups=mesh['src_0'=4,'src_1'=4,'rcv_0'=4,'rcv_1'=2] {'rcv_0','rcv_1'}, dimensions={0} | all-to-all | bytes 4194304 | tf_op jit(solution)/shard_map/all_to_all | solution.py:24
  369.5 7.9 %fusion.59 = f32[2,128,256]{2,1,0:T(8,128)S(1)} fusion(s32[256]{0:T(256)S(1)} %iota_add_fusion, bf16[2,2,128,2048]{3,2,0,1:T(8,128)(2,1)S(1)} %bitcast.296), kind=kOutput, calls=%fused_computation.103 | convolution fusion | flops 276824064 | bytes 1311744 | tf_op jit(solution)/shard_map/fmn,nc->fmc/dot_general | solution.py:91
  377.4 8.3 %fusion.70 = f32[2,128,256]{2,1,0:T(8,128)S(1)} fusion(s32[256]{0:T(256)S(1)} %iota_add_fusion, bf16[2,2,128,2048]{3,2,0,1:T(8,128)(2,1)S(1)} %bitcast.297), kind=kOutput, calls=%fused_computation.107 | convolution fusion | flops 276824064 | bytes 1311744 | tf_op jit(solution)/shard_map/fmn,nc->fmc/dot_general | solution.py:91
  385.7 8.1 %fusion.42 = bf16[2,1,128,256]{3,2,0,1:T(8,128)(2,1)S(1)} fusion(f32[2,128,256]{2,1,0:T(8,128)S(1)} %fusion.59, s32[256]{0:T(256)S(1)} %iota_add_fusion, bf16[2,2,128,2048]{3,2,0,1:T(8,128)(2,1)S(1)} %bitcast.298), kind=kOutput, calls=%fused_computation.78 | convolution fusion | flops 276955136 | bytes 1442816 | tf_op jit(solution)/shard_map/fmn,nc->fmc/dot_general | solution.py:91
  393.9 7.9 %fusion.41 = bf16[2,1,128,256]{3,2,0,1:T(8,128)(2,1)S(1)} fusion(f32[2,128,256]{2,1,0:T(8,128)S(1)} %fusion.70, s32[256]{0:T(256)S(1)} %iota_add_fusion, bf16[2,2,128,2048]{3,2,0,1:T(8,128)(2,1)S(1)} %bitcast.299), kind=kOutput, calls=%fused_computation.77 | convolution fusion | flops 276955136 | bytes 1442816 | tf_op jit(solution)/shard_map/fmn,nc->fmc/dot_general | solution.py:91
  402.0 29.7 %all_to_all.11 = bf16[8,2,2,128,256]{4,3,1,2,0:T(8,128)(2,1)S(1)} all-to-all(bf16[8,2,2,128,256]{4,3,1,2,0:T(8,128)(2,1)S(1)} %broadcast_in_dim.5), channel_id=1, replica_groups=mesh['src_0'=4,'src_1'=4,'rcv_0'=4,'rcv_1'=2] {'rcv_0','rcv_1'}, dimensions={0} | all-to-all | bytes 4194304 | tf_op jit(solution)/shard_map/all_to_all | solution.py:24
  432.0 1.9 copy-done.1
  439.9 2.7 maximum_subtract_fusion.1
  442.6 56.6 %all-reduce.3 = bf16[2,2,128,2048]{3,2,0,1:T(8,128)(2,1)S(1)} all-reduce(f32[2,2,128,2048]{3,2,0,1:T(8,128)} %maximum_subtract_fusion.1), channel_id=1, replica_groups=mesh['src_0'=4,'src_1'=4,'rcv_0'=4,'rcv_1'=2] {'rcv_0','rcv_1'}, use_global_device_ids=true, to_apply=%region_3.4 | all-reduce | flops 1048576 | bytes 6291456 | tf_op jit(solution)/shard_map/psum | solution.py:163
  499.2 7.9 %fusion.56 = f32[2,128,256]{2,1,0:T(8,128)S(1)} fusion(s32[256]{0:T(256)S(1)} %iota_add_fusion, bf16[2,2,128,2048]{3,2,0,1:T(8,128)(2,1)S(1)} %all-reduce.3), kind=kOutput, calls=%fused_computation.102 | convolution fusion | flops 276824064 | bytes 1311744 | tf_op jit(solution)/shard_map/fmn,nc->fmc/dot_general | solution.py:91
  507.1 8.1 %fusion.64 = f32[2,128,256]{2,1,0:T(8,128)S(1)} fusion(s32[256]{0:T(256)S(1)} %iota_add_fusion, bf16[2,2,128,2048]{3,2,0,1:T(8,128)(2,1)S(1)} %all-reduce.3), kind=kOutput, calls=%fused_computation.105 | convolution fusion | flops 276824064 | bytes 1311744 | tf_op jit(solution)/shard_map/fmn,nc->fmc/dot_general | solution.py:91
  515.2 8.2 %fusion.40 = bf16[2,1,128,256]{3,2,0,1:T(8,128)(2,1)S(1)} fusion(f32[2,128,256]{2,1,0:T(8,128)S(1)} %fusion.56, s32[256]{0:T(256)S(1)} %iota_add_fusion, bf16[2,2,128,2048]{3,2,0,1:T(8,128)(2,1)S(1)} %all-reduce.3), kind=kOutput, calls=%fused_computation.76 | convolution fusion | flops 276955136 | bytes 1442816 | tf_op jit(solution)/shard_map/fmn,nc->fmc/dot_general | solution.py:91
  523.4 7.9 %fusion.39 = bf16[2,1,128,256]{3,2,0,1:T(8,128)(2,1)S(1)} fusion(f32[2,128,256]{2,1,0:T(8,128)S(1)} %fusion.64, s32[256]{0:T(256)S(1)} %iota_add_fusion, bf16[2,2,128,2048]{3,2,0,1:T(8,128)(2,1)S(1)} %all-reduce.3), kind=kOutput, calls=%fused_computation.75 | convolution fusion | flops 276955136 | bytes 1442816 | tf_op jit(solution)/shard_map/fmn,nc->fmc/dot_general | solution.py:91
  532.0 51.3 %all-gather.27.cloned.1.call-done = bf16[2,2,2048,256]{3,2,0,1:T(8,128)(2,1)} async-done(((bf16[2,2,128,256]{3,2,0,1:T(8,128)(2,1)}), bf16[2,2,2048,256]{3,2,0,1:T(8,128)(2,1)}) %all-gather.27.cloned.1.call-update) | async-done | bytes 4194320 | tf_op jit(solution)/shard_map/all_gather | solution.py:167
  583.3 6.4 fusion.16
  589.7 4.3 fusion.15
  594.0 4.3 fusion.20
  598.3 4.5 fusion.22
  603.1 7.6 %all-gather.12 = f32[4,2,2]{2,1,0:T(2,128)S(1)} all-gather(f32[1,2,2]{2,1,0:T(2,128)S(1)} %maximum_bitcast_fusion.5), channel_id=6, replica_groups=mesh['src_0'=4,'src_1'=4,'rcv_0'=4,'rcv_1'=2] {'src_0'}, dimensions={0}, use_global_device_ids=true | all-gather | bytes 80 | tf_op jit(solution)/shard_map/all_gather | solution.py:39
  610.8 5.9 all-gather.13
  616.7 7.8 %all-gather.14 = f32[4,2,2]{2,1,0:T(2,128)S(1)} all-gather(f32[1,2,2]{2,1,0:T(2,128)S(1)} %maximum_bitcast_fusion.7), channel_id=8, replica_groups=mesh['src_0'=4,'src_1'=4,'rcv_0'=4,'rcv_1'=2] {'rcv_0'}, dimensions={0}, use_global_device_ids=true | all-gather | bytes 80 | tf_op jit(solution)/shard_map/all_gather | solution.py:39
  624.5 8.2 %all-gather.15 = f32[2,2,2]{2,1,0:T(2,128)S(1)} all-gather(f32[1,2,2]{2,1,0:T(2,128)S(1)} %maximum_bitcast_fusion.8), channel_id=9, replica_groups=mesh['src_0'=4,'src_1'=4,'rcv_0'=4,'rcv_1'=2] {'rcv_1'}, dimensions={0}, use_global_device_ids=true | all-gather | bytes 48 | tf_op jit(solution)/shard_map/all_gather | solution.py:39
  633.0 1.0 copy.35
  (70 shorter events, 15.9 us)
Async XLA Ops:
  7.2 58.1 %all-gather.21.cloned.1.call-start = ((), (), s32[]{:S(2)}) async-start(), calls=%async_computation.2 | async-start | bytes 4456448 | tf_op jit(solution)/shard_map/all_gather | solution.py:126
  8.9 207.7 %all-gather.23.cloned.1.call-start = ((), (), s32[]{:S(2)}) async-start(), calls=%async_computation.3 | async-start | bytes 4456448 | tf_op jit(solution)/shard_map/all_gather | solution.py:167
  10.0 2.5 copy-start.2
  65.3 2.8 copy-start
  165.1 151.9 %all-gather.25.cloned.1.call-start = ((), (), s32[]{:S(2)}) async-start(), calls=%async_computation.4 | async-start | bytes 4456448 | tf_op jit(solution)/shard_map/all_gather | solution.py:142
  216.7 6.0 copy-start.3
  266.5 316.8 %all-gather.27.cloned.1.call-start = ((), (), s32[]{:S(2)}) async-start(), calls=%async_computation.5 | async-start | bytes 4456448 | tf_op jit(solution)/shard_map/all_gather | solution.py:167
  317.0 6.1 copy-start.4
  431.7 2.2 copy-start.1
  583.3 6.4 %copy-start.5 = (bf16[2,2,2048,256]{3,2,0,1:T(8,128)(2,1)S(1)}, bf16[2,2,2048,256]{3,2,0,1:T(8,128)(2,1)}, u32[]{:S(2)}) copy-start(bf16[2,2,2048,256]{3,2,0,1:T(8,128)(2,1)} %all-gather.27.cloned.1.call-done) | copy-start | bytes 12582916
Sparse Core Ops, SparseCore 0:
  10.7 54.5 all-gather.20
  165.2 51.4 all-gather.22
  266.6 50.2 all-gather.24
  532.2 51.0 all-gather.26
where the time goes:
time: 645 us; the launch traced here: 641 us
  blocking collectives  234 us (36%)
  waiting for transfers between devices  204 us (32%)
  matrix products  165 us (26%)
  between operations  14.4 us (2%)
  other arithmetic  13.8 us (2%)
  local copies, waits for them, and re-layouts  9 us (1%)
    dot_general x28, matrix products, single(): jnp.einsum(pattern, first_op, second_op, preferred_element_type=jnp.float32)  156 us
    psum x2, blocking collectives, per_device(): gradient_rows = lax.psum(embedded - scaled, RCV)  113 us
    all_gather x2, waiting for transfers between devices, per_device(): lax.all_gather(halfway, SRC, axis=2, tiled=True)  102 us
    all_to_all x2, blocking collectives, copy_for_each(): return lax.all_to_all(copies, axis, split_axis=0, concat_axis=0, tiled=True)  61.9 us
    all_gather x8, blocking collectives, all_in_one(): both, at, found = (lax.all_gather(jnp.concatenate(lines), axis), 0, {})  59 us
    all_gather x1, waiting for transfers between devices, per_device(): columns_all = lax.all_gather(traces, SRC, axis=2, tiled=True)  51.9 us
    all_gather x1, waiting for transfers between devices, per_device(): lax.all_gather(coeff_half, SRC, axis=2, tiled=True)  50 us
  transfers between devices with their start and end apart: 4, of which 4 were waited for; matrix products, arithmetic and copies ran while one was open for 1% of the time, Pallas kernels for 0%

commit v1 on v0

--- a/solution.py
+++ b/solution.py
@@ -11,6 +11,9 @@
 SRC_RCV = ("src_0", "src_1", "rcv_0", "rcv_1")
 step_length = 0.4
 shrink_fraction = 0.2
+hold_tails_by_axis = lambda here_x: jnp.concatenate(
+    lax.all_to_all(jnp.stack(lax.psum(1, SRC) * [here_x], 0), SRC, 0, 0), 2
+)
 
 
 def laid_out(tiles, dim):
@@ -138,9 +141,9 @@
             misfit = traces_f
         else:
             coeff_half = coeffs.astype(jnp.bfloat16)
-            halfway = column_section(
-                inverse_rows, lax.all_gather(coeff_half, SRC, axis=2, tiled=True)
-            ).astype(jnp.bfloat16)
+            halfway = column_section(inverse_rows, hold_tails_by_axis(coeff_half)).astype(
+                jnp.bfloat16
+            )
             model = complex_product(
                 gathered_copies(halfway, RCV, 3), inverse_cols, "fmn,nc->fmc", False, True
             ).astype(jnp.bfloat16)

time: 645 us -> 643 us (level)
  waiting for transfers between devices: 204 us -> 152 us
  blocking collectives: 234 us -> 285 us
    all_to_all x0 -> x1, blocking collectives: none -> 53.3 us  [lax.all_to_all(jnp.stack(lax.psum(1, SRC) * [here_x], 0), SRC, 0, 0)]
    all_gather x1 -> x0, waiting for transfers between devices: 50 us -> none  [per_device(): lax.all_gather(coeff_half, SRC, axis=2, tiled=True)]
  transfers between devices with their start and end apart: 4 -> 3, of which waited for: 4 -> 3; matrix products, arithmetic and copies ran while one was open for 1% -> 1% of each run, Pallas kernels for 0% -> 0%
where the time goes in v1:
time: 643 us; the launch traced here: 639 us
  blocking collectives  285 us (44%)
  matrix products  163 us (25%)
  waiting for transfers between devices  152 us (24%)
  between operations  14.3 us (2%)
  other arithmetic  13.1 us (2%)
  local copies, waits for them, and re-layouts  10.6 us (2%)
    dot_general x28, matrix products, single(): jnp.einsum(pattern, first_op, second_op, preferred_element_type=jnp.float32)  155 us
    psum x2, blocking collectives, per_device(): gradient_rows = lax.psum(embedded - scaled, RCV)  113 us
    all_gather x2, waiting for transfers between devices, per_device(): lax.all_gather(halfway, SRC, axis=2, tiled=True)  100 us
    all_to_all x2, blocking collectives, copy_for_each(): return lax.all_to_all(copies, axis, split_axis=0, concat_axis=0, tiled=True)  59.8 us
    all_gather x8, blocking collectives, all_in_one(): both, at, found = (lax.all_gather(jnp.concatenate(lines), axis), 0, {})  59 us
    all_to_all x1, blocking collectives, lax.all_to_all(jnp.stack(lax.psum(1, SRC) * [here_x], 0), SRC, 0, 0)  53.3 us
    all_gather x1, waiting for transfers between devices, per_device(): columns_all = lax.all_gather(traces, SRC, axis=2, tiled=True)  51.9 us
  transfers between devices with their start and end apart: 3, of which 3 were waited for; matrix products, arithmetic and copies ran while one was open for 1% of the time, Pallas kernels for 0%

profile of v1, /device:TPU:1, one launch (start us, length us, event | category | flops | bytes accessed | tf_op | source)
XLA Modules:
  0.0 639.0 jit_solution(542015962226861982)
XLA Ops:
  7.2 1.7 copy.19
  10.0 2.5 broadcast.429.clone
  13.3 51.9 %all-gather.20.cloned.1.call-done = bf16[2,2,2048,256]{3,2,0,1:T(8,128)(2,1)} async-done(((bf16[2,2,128,256]{3,2,0,1:T(8,128)(2,1)}), bf16[2,2,2048,256]{3,2,0,1:T(8,128)(2,1)}) %all-gather.20.cloned.1.call-update) | async-done | bytes 4194320 | tf_op jit(solution)/shard_map/all_gather | solution.py:129
  65.3 2.5 fusion.78
  70.7 5.0 maximum_subtract_fusion
  75.7 56.5 %all-reduce.2 = bf16[2,2,128,2048]{3,2,0,1:T(8,128)(2,1)S(1)} all-reduce(f32[2,2,128,2048]{3,2,0,1:T(8,128)} %maximum_subtract_fusion), channel_id=1, replica_groups=mesh['src_0'=4,'src_1'=4,'rcv_0'=4,'rcv_1'=2] {'rcv_0','rcv_1'}, use_global_device_ids=true, to_apply=%region_0.1 | all-reduce | flops 1048576 | bytes 6291456 | tf_op jit(solution)/shard_map/psum | solution.py:166
  132.2 7.9 %fusion.62 = f32[2,128,256]{2,1,0:T(8,128)S(1)} fusion(s32[256]{0:T(256)S(1)} %iota_add_fusion, bf16[2,2,128,2048]{3,2,0,1:T(8,128)(2,1)S(1)} %all-reduce.2), kind=kOutput, calls=%fused_computation.105 | convolution fusion | flops 276824064 | bytes 1311744 | tf_op jit(solution)/shard_map/fmn,nc->fmc/dot_general | solution.py:94
  140.1 8.1 %fusion.67 = f32[2,128,256]{2,1,0:T(8,128)S(1)} fusion(s32[256]{0:T(256)S(1)} %iota_add_fusion, bf16[2,2,128,2048]{3,2,0,1:T(8,128)(2,1)S(1)} %all-reduce.2), kind=kOutput, calls=%fused_computation.107 | convolution fusion | flops 276824064 | bytes 1311744 | tf_op jit(solution)/shard_map/fmn,nc->fmc/dot_general | solution.py:94
  148.2 8.2 %fusion.44 = bf16[2,1,128,256]{3,2,0,1:T(8,128)(2,1)S(1)} fusion(f32[2,128,256]{2,1,0:T(8,128)S(1)} %fusion.62, s32[256]{0:T(256)S(1)} %iota_add_fusion, bf16[2,2,128,2048]{3,2,0,1:T(8,128)(2,1)S(1)} %all-reduce.2), kind=kOutput, calls=%fused_computation.81 | convolution fusion | flops 276955136 | bytes 1442816 | tf_op jit(solution)/shard_map/fmn,nc->fmc/dot_general | solution.py:94
  156.4 7.9 %fusion.43 = bf16[2,1,128,256]{3,2,0,1:T(8,128)(2,1)S(1)} fusion(f32[2,128,256]{2,1,0:T(8,128)S(1)} %fusion.67, s32[256]{0:T(256)S(1)} %iota_add_fusion, bf16[2,2,128,2048]{3,2,0,1:T(8,128)(2,1)S(1)} %all-reduce.2), kind=kOutput, calls=%fused_computation.80 | convolution fusion | flops 276955136 | bytes 1442816 | tf_op jit(solution)/shard_map/fmn,nc->fmc/dot_general | solution.py:94
  165.5 51.1 %all-gather.22.cloned.1.call-done = bf16[2,2,2048,256]{3,2,0,1:T(8,128)(2,1)} async-done(((bf16[2,2,128,256]{3,2,0,1:T(8,128)(2,1)}), bf16[2,2,2048,256]{3,2,0,1:T(8,128)(2,1)}) %all-gather.22.cloned.1.call-update) | async-done | bytes 4194320 | tf_op jit(solution)/shard_map/all_gather | solution.py:170
  216.6 6.0 fusion.8
  222.7 4.3 fusion.7
  227.0 4.5 fusion.26
  231.5 4.3 fusion.28
  236.0 7.6 %all-gather.8 = f32[4,2,2]{2,1,0:T(2,128)S(1)} all-gather(f32[1,2,2]{2,1,0:T(2,128)S(1)} %maximum_bitcast_fusion.1), channel_id=2, replica_groups=mesh['src_0'=4,'src_1'=4,'rcv_0'=4,'rcv_1'=2] {'src_0'}, dimensions={0}, use_global_device_ids=true | all-gather | bytes 80 | tf_op jit(solution)/shard_map/all_gather | solution.py:42
  243.7 5.9 all-gather.9
  249.5 7.8 %all-gather.10 = f32[4,2,2]{2,1,0:T(2,128)S(1)} all-gather(f32[1,2,2]{2,1,0:T(2,128)S(1)} %maximum_bitcast_fusion.3), channel_id=4, replica_groups=mesh['src_0'=4,'src_1'=4,'rcv_0'=4,'rcv_1'=2] {'rcv_0'}, dimensions={0}, use_global_device_ids=true | all-gather | bytes 80 | tf_op jit(solution)/shard_map/all_gather | solution.py:42
  257.4 8.2 %all-gather.11 = f32[2,2,2]{2,1,0:T(2,128)S(1)} all-gather(f32[1,2,2]{2,1,0:T(2,128)S(1)} %maximum_bitcast_fusion.4), channel_id=5, replica_groups=mesh['src_0'=4,'src_1'=4,'rcv_0'=4,'rcv_1'=2] {'rcv_1'}, dimensions={0}, use_global_device_ids=true | all-gather | bytes 48 | tf_op jit(solution)/shard_map/all_gather | solution.py:42
  265.8 1.0 stack.142
  266.8 53.3 %all_to_all.15 = bf16[16,2,2,128,256]{3,4,1,2,0:T(8,128)(2,1)S(1)} all-to-all(bf16[16,2,2,128,256]{3,4,1,2,0:T(8,128)(2,1)S(1)} %stack.142), channel_id=1, replica_groups=mesh['src_0'=4,'src_1'=4,'rcv_0'=4,'rcv_1'=2] {'src_0','src_1'}, dimensions={0} | all-to-all | bytes 8388608 | tf_op jit(solution)/shard_map/all_to_all | solution.py:15
  320.7 4.4 fusion.12
  325.1 4.4 fusion.11
  329.5 4.6 fusion.37
  334.0 4.4 fusion.38
  338.9 30.1 %all_to_all.16 = bf16[8,2,2,128,256]{4,3,1,2,0:T(8,128)(2,1)S(1)} all-to-all(bf16[8,2,2,128,256]{4,3,1,2,0:T(8,128)(2,1)S(1)} %broadcast_in_dim.4), channel_id=1, replica_groups=mesh['src_0'=4,'src_1'=4,'rcv_0'=4,'rcv_1'=2] {'rcv_0','rcv_1'}, dimensions={0} | all-to-all | bytes 4194304 | tf_op jit(solution)/shard_map/all_to_all | solution.py:27
  369.3 7.9 %fusion.59 = f32[2,128,256]{2,1,0:T(8,128)S(1)} fusion(s32[256]{0:T(256)S(1)} %iota_add_fusion, bf16[2,2,128,2048]{3,2,0,1:T(8,128)(2,1)S(1)} %bitcast.302), kind=kOutput, calls=%fused_computation.104 | convolution fusion | flops 276824064 | bytes 1311744 | tf_op jit(solution)/shard_map/fmn,nc->fmc/dot_general | solution.py:94
  377.2 8.4 %fusion.70 = f32[2,128,256]{2,1,0:T(8,128)S(1)} fusion(s32[256]{0:T(256)S(1)} %iota_add_fusion, bf16[2,2,128,2048]{3,2,0,1:T(8,128)(2,1)S(1)} %bitcast.303), kind=kOutput, calls=%fused_computation.108 | convolution fusion | flops 276824064 | bytes 1311744 | tf_op jit(solution)/shard_map/fmn,nc->fmc/dot_general | solution.py:94
  385.5 8.1 %fusion.42 = bf16[2,1,128,256]{3,2,0,1:T(8,128)(2,1)S(1)} fusion(f32[2,128,256]{2,1,0:T(8,128)S(1)} %fusion.59, s32[256]{0:T(256)S(1)} %iota_add_fusion, bf16[2,2,128,2048]{3,2,0,1:T(8,128)(2,1)S(1)} %bitcast.304), kind=kOutput, calls=%fused_computation.79 | convolution fusion | flops 276955136 | bytes 1442816 | tf_op jit(solution)/shard_map/fmn,nc->fmc/dot_general | solution.py:94
  393.7 7.9 %fusion.41 = bf16[2,1,128,256]{3,2,0,1:T(8,128)(2,1)S(1)} fusion(f32[2,128,256]{2,1,0:T(8,128)S(1)} %fusion.70, s32[256]{0:T(256)S(1)} %iota_add_fusion, bf16[2,2,128,2048]{3,2,0,1:T(8,128)(2,1)S(1)} %bitcast.305), kind=kOutput, calls=%fused_computation.78 | convolution fusion | flops 276955136 | bytes 1442816 | tf_op jit(solution)/shard_map/fmn,nc->fmc/dot_general | solution.py:94
  401.8 29.7 %all_to_all.17 = bf16[8,2,2,128,256]{4,3,1,2,0:T(8,128)(2,1)S(1)} all-to-all(bf16[8,2,2,128,256]{4,3,1,2,0:T(8,128)(2,1)S(1)} %broadcast_in_dim.5), channel_id=1, replica_groups=mesh['src_0'=4,'src_1'=4,'rcv_0'=4,'rcv_1'=2] {'rcv_0','rcv_1'}, dimensions={0} | all-to-all | bytes 4194304 | tf_op jit(solution)/shard_map/all_to_all | solution.py:27
  431.8 1.9 copy-done.1
  439.8 2.7 maximum_subtract_fusion.1
  442.5 56.6 %all-reduce.3 = bf16[2,2,128,2048]{3,2,0,1:T(8,128)(2,1)S(1)} all-reduce(f32[2,2,128,2048]{3,2,0,1:T(8,128)} %maximum_subtract_fusion.1), channel_id=1, replica_groups=mesh['src_0'=4,'src_1'=4,'rcv_0'=4,'rcv_1'=2] {'rcv_0','rcv_1'}, use_global_device_ids=true, to_apply=%region_3.4 | all-reduce | flops 1048576 | bytes 6291456 | tf_op jit(solution)/shard_map/psum | solution.py:166
  499.0 7.9 %fusion.56 = f32[2,128,256]{2,1,0:T(8,128)S(1)} fusion(s32[256]{0:T(256)S(1)} %iota_add_fusion, bf16[2,2,128,2048]{3,2,0,1:T(8,128)(2,1)S(1)} %all-reduce.3), kind=kOutput, calls=%fused_computation.103 | convolution fusion | flops 276824064 | bytes 1311744 | tf_op jit(solution)/shard_map/fmn,nc->fmc/dot_general | solution.py:94
  506.9 8.1 %fusion.64 = f32[2,128,256]{2,1,0:T(8,128)S(1)} fusion(s32[256]{0:T(256)S(1)} %iota_add_fusion, bf16[2,2,128,2048]{3,2,0,1:T(8,128)(2,1)S(1)} %all-reduce.3), kind=kOutput, calls=%fused_computation.106 | convolution fusion | flops 276824064 | bytes 1311744 | tf_op jit(solution)/shard_map/fmn,nc->fmc/dot_general | solution.py:94
  515.0 8.2 %fusion.40 = bf16[2,1,128,256]{3,2,0,1:T(8,128)(2,1)S(1)} fusion(f32[2,128,256]{2,1,0:T(8,128)S(1)} %fusion.56, s32[256]{0:T(256)S(1)} %iota_add_fusion, bf16[2,2,128,2048]{3,2,0,1:T(8,128)(2,1)S(1)} %all-reduce.3), kind=kOutput, calls=%fused_computation.77 | convolution fusion | flops 276955136 | bytes 1442816 | tf_op jit(solution)/shard_map/fmn,nc->fmc/dot_general | solution.py:94
  523.2 7.9 %fusion.39 = bf16[2,1,128,256]{3,2,0,1:T(8,128)(2,1)S(1)} fusion(f32[2,128,256]{2,1,0:T(8,128)S(1)} %fusion.64, s32[256]{0:T(256)S(1)} %iota_add_fusion, bf16[2,2,128,2048]{3,2,0,1:T(8,128)(2,1)S(1)} %all-reduce.3), kind=kOutput, calls=%fused_computation.76 | convolution fusion | flops 276955136 | bytes 1442816 | tf_op jit(solution)/shard_map/fmn,nc->fmc/dot_general | solution.py:94
  531.9 49.2 %all-gather.24.cloned.1.call-done = bf16[2,2,2048,256]{3,2,0,1:T(8,128)(2,1)} async-done(((bf16[2,2,128,256]{3,2,0,1:T(8,128)(2,1)}), bf16[2,2,2048,256]{3,2,0,1:T(8,128)(2,1)}) %all-gather.24.cloned.1.call-update) | async-done | bytes 4194320 | tf_op jit(solution)/shard_map/all_gather | solution.py:170
  581.1 6.4 %fusion.16 = f32[2,256,128]{2,1,0:T(8,128)S(1)} fusion(bf16[2,2,2048,256]{3,2,0,1:T(8,128)(2,1)} %all-gather.24.cloned.1.call-done, s32[128]{0:T(128)S(1)} %iota_add_fusion.1), kind=kOutput, calls=%fused_computation.42 | convolution fusion | flops 272629760 | bytes 2359808 | tf_op jit(solution)/shard_map/mn,fnc->fmc/dot_general | solution.py:94
  587.5 4.3 fusion.15
  591.8 4.3 fusion.20
  596.1 4.4 fusion.22
  600.9 7.6 %all-gather.12 = f32[4,2,2]{2,1,0:T(2,128)S(1)} all-gather(f32[1,2,2]{2,1,0:T(2,128)S(1)} %maximum_bitcast_fusion.5), channel_id=6, replica_groups=mesh['src_0'=4,'src_1'=4,'rcv_0'=4,'rcv_1'=2] {'src_0'}, dimensions={0}, use_global_device_ids=true | all-gather | bytes 80 | tf_op jit(solution)/shard_map/all_gather | solution.py:42
  608.5 5.9 all-gather.13
  614.4 7.8 %all-gather.14 = f32[4,2,2]{2,1,0:T(2,128)S(1)} all-gather(f32[1,2,2]{2,1,0:T(2,128)S(1)} %maximum_bitcast_fusion.7), channel_id=8, replica_groups=mesh['src_0'=4,'src_1'=4,'rcv_0'=4,'rcv_1'=2] {'rcv_0'}, dimensions={0}, use_global_device_ids=true | all-gather | bytes 80 | tf_op jit(solution)/shard_map/all_gather | solution.py:42
  622.3 8.2 %all-gather.15 = f32[2,2,2]{2,1,0:T(2,128)S(1)} all-gather(f32[1,2,2]{2,1,0:T(2,128)S(1)} %maximum_bitcast_fusion.8), channel_id=9, replica_groups=mesh['src_0'=4,'src_1'=4,'rcv_0'=4,'rcv_1'=2] {'rcv_1'}, dimensions={0}, use_global_device_ids=true | all-gather | bytes 48 | tf_op jit(solution)/shard_map/all_gather | solution.py:42
  630.7 1.0 copy.36
  (68 shorter events, 16.4 us)
Async XLA Ops:
  7.2 58.1 %all-gather.20.cloned.1.call-start = ((), (), s32[]{:S(2)}) async-start(), calls=%async_computation.3 | async-start | bytes 4456448 | tf_op jit(solution)/shard_map/all_gather | solution.py:129
  8.9 207.7 %all-gather.22.cloned.1.call-start = ((), (), s32[]{:S(2)}) async-start(), calls=%async_computation.4 | async-start | bytes 4456448 | tf_op jit(solution)/shard_map/all_gather | solution.py:170
  10.0 2.5 copy-start.2
  65.3 2.8 copy-start
  165.1 416.0 %all-gather.24.cloned.1.call-start = ((), (), s32[]{:S(2)}) async-start(), calls=%async_computation.5 | async-start | bytes 4456448 | tf_op jit(solution)/shard_map/all_gather | solution.py:170
  216.6 6.0 copy-start.3
  431.5 2.2 copy-start.1
  581.1 6.4 %copy-start.4 = (bf16[2,2,2048,256]{3,2,0,1:T(8,128)(2,1)S(1)}, bf16[2,2,2048,256]{3,2,0,1:T(8,128)(2,1)}, u32[]{:S(2)}) copy-start(bf16[2,2,2048,256]{3,2,0,1:T(8,128)(2,1)} %all-gather.24.cloned.1.call-done) | copy-start | bytes 12582916
Sparse Core Ops, SparseCore 0:
  10.7 54.5 all-gather.19
  165.2 51.4 all-gather.21
  532.0 49.0 all-gather.23
